TPU v7x, 512 devices: a whole 4x8x8 slice. The times are simulated.
512 devices in a mesh: frame: 32 (over y_lo, z, core), space: 16 (over x, y_hi).
Axes of the slice: x: 4, y: 8 (y_hi: 4, y_lo: 2; y = y_hi * 2 + y_lo), z: 8, core: 2. Of those that a mesh axis runs over, the one named last changes fastest.
Arguments:
- spatial_query: bfloat16 [32, 1024, 1152], P('frame', 'space'), may hold values from -24 to 24
- spatial_key: bfloat16 [32, 1024, 1152], P('frame', 'space'), may hold values from -24 to 24
- spatial_value: bfloat16 [32, 1024, 1152], P('frame', 'space'), may hold values from -6 to 6
- latents: bfloat16 [32, 1024, 1152], P('frame', 'space'), may hold values from -6 to 6
- proj_weight: bfloat16 [1152, 1152], P('frame'), may hold values from -0.1875 to 0.1875
- proj_bias: float32 [1152], replicated, may hold values from -3 to 3
- residual_gate: float32 [1152], replicated, may hold values from 0.5 to 1.5
- temporal_shift: float32 [1152], replicated, may hold values from -3 to 3
- temporal_scale: float32 [1152], replicated, may hold values from -0.5 to 0.5
- temporal_weight: bfloat16 [1152, 3456], P('frame'), may hold values from -0.75 to 0.75
- clip_lengths: int32 [16], replicated, may hold values from 1 to 4, 32 in all
Outputs:
- hidden: float32 [32, 1024, 1152], P('frame', 'space')
- temporal_out: float32 [32, 1024, 1152], P('frame', 'space')
Inputs may be any that keep to these rules, and one draw needn't show every extreme that they name: `clip_lengths`: 16 clips fill the 32 frames in order; one clip has exactly 4 frames.
All inputs are finite; a program needn't handle non-finite values.
Results may differ from a plain program's by a relative error of at most 0.012.
Values may be sent and summed in bfloat16 or wider, within the bound.
A program may use at most 64 MiB of HBM per device.

v0:
```python
import math
import jax
import jax.numpy as jnp
from jax import lax
from jax.sharding import Mesh
from jax.sharding import PartitionSpec as P

HEADS = 16
FRAME = ("frame_0", "frame_1", "frame_2")
neg_fill = -1e30


def in_blocks(shard, dim, devices):
    before, after = (shard.shape[:dim], shard.shape[dim + 1 :])
    return jnp.moveaxis(shard.reshape(*before, devices, -1, *after), dim, 0)


def in_order(blocks, dim):
    shape = list(blocks.shape[1:])
    shape[dim] *= blocks.shape[0]
    return jnp.moveaxis(blocks, 0, dim).reshape(shape)


def exchange_in_order(blocks, axes, sequence):
    shape = [lax.axis_size(a) for a in axes]
    blocks = blocks.reshape(*shape, *blocks.shape[1:])
    for k in sequence:
        blocks = lax.all_to_all(blocks, axes[k], split_axis=k, concat_axis=k, tiled=True)
    return blocks.reshape(-1, *blocks.shape[len(axes) :])


def exchange_by_chip(shard, groups, sequence, split_dim, concat_dim):
    devices = lax.axis_size(groups[0]) * lax.axis_size(groups[1])
    blocks = in_blocks(shard, split_dim, devices)
    return in_order(exchange_in_order(blocks, groups, sequence), concat_dim)


def head_scores(query, keys):
    factor = 1.0 / math.sqrt(query.shape[-1])
    return jnp.einsum("fahd,fbhd->fhab", query, keys, preferred_element_type=jnp.float32) * factor


def frame_attention(parts):
    query, keys, values = parts
    frames, count, heads, head_dim = query.shape
    block = math.gcd(count, 512)
    blocks = jnp.moveaxis(query.reshape(frames, count // block, block, heads, head_dim), 1, 0)

    def one_block(rows):
        scores = head_scores(rows, keys)
        top = jnp.max(scores, axis=-1, keepdims=True)
        probs = jnp.exp(scores - top)
        total = jnp.sum(probs, axis=-1)
        mixed = jnp.einsum(
            "fhab,fbhd->fahd",
            probs.astype(jnp.bfloat16),
            values,
            preferred_element_type=jnp.float32,
        )
        return (mixed / jnp.transpose(total, (0, 2, 1))[..., None]).astype(jnp.bfloat16)

    result = lax.map(one_block, blocks)
    return jnp.moveaxis(result, 0, 1).reshape(frames, count, heads, head_dim)


def temporal_mix(packed, allowed):
    frames, count = (packed.shape[0], packed.shape[1])
    width = packed.shape[2] // 3
    head_dim = width // HEADS
    split = (frames, count, HEADS, head_dim)
    query = packed[:, :, :width].reshape(split)
    keys = packed[:, :, width : 2 * width].reshape(split)
    values = packed[:, :, 2 * width :].reshape(split)
    scores = jnp.einsum("anhd,bnhd->nhab", query, keys, preferred_element_type=jnp.float32) * (
        1.0 / math.sqrt(head_dim)
    )
    scores = jnp.where(allowed, scores, neg_fill)
    top = jnp.max(scores, axis=-1, keepdims=True)
    probs = jnp.exp(scores - top)
    total = jnp.sum(probs, axis=-1)
    mixed = jnp.einsum(
        "nhab,bnhd->anhd", probs.astype(jnp.bfloat16), values, preferred_element_type=jnp.float32
    )
    mixed = mixed / jnp.transpose(total, (2, 0, 1))[..., None]
    return mixed.reshape(frames, count, width)


def shards(
    spatial_query,
    spatial_key,
    spatial_value,
    latents,
    proj_weight,
    proj_bias,
    residual_gate,
    temporal_shift,
    temporal_scale,
    temporal_weight,
    clip_lengths,
):
    frames_dev, patches_dev, width = latents.shape
    head_dim = width // HEADS
    split = (frames_dev, patches_dev, HEADS, head_dim)
    query = spatial_query.reshape(split)
    mixed_heads = frame_attention(
        (
            lax.all_to_all(query, "space", split_axis=2, concat_axis=1, tiled=True),
            lax.all_to_all(
                spatial_key.reshape(split), "space", split_axis=2, concat_axis=1, tiled=True
            ),
            lax.all_to_all(
                spatial_value.reshape(split), "space", split_axis=2, concat_axis=1, tiled=True
            ),
        )
    )
    attended = lax.all_to_all(mixed_heads, "space", split_axis=1, concat_axis=2, tiled=True)
    rows = frames_dev * patches_dev
    flat = attended.reshape(rows, width)
    projected = jnp.dot(
        flat,
        lax.all_gather(proj_weight, FRAME, axis=0, tiled=True),
        preferred_element_type=jnp.float32,
    )
    hidden = latents.reshape(rows, width).astype(jnp.float32) + residual_gate * (
        projected + proj_bias
    )
    mean = jnp.mean(hidden, axis=-1, keepdims=True)
    centred = hidden - mean
    variance = jnp.mean(centred * centred, axis=-1, keepdims=True)
    normed = (
        centred * lax.rsqrt(variance + 1e-06) * (1.0 + temporal_scale) + temporal_shift
    ).astype(jnp.bfloat16)
    groups = lax.axis_size(FRAME)
    frames_all = frames_dev * groups
    per_group = patches_dev // groups
    ends = jnp.cumsum(clip_lengths)
    clip_of = jnp.sum(
        (jnp.arange(frames_all, dtype=jnp.int32)[:, None] >= ends[None, :]).astype(jnp.int32),
        axis=1,
    )
    allowed = clip_of[:, None] == clip_of[None, :]
    whole_weight = lax.all_gather(temporal_weight, FRAME, axis=0, tiled=True)
    local = jnp.einsum(
        "fnc,ce->fne",
        exchange_by_chip(
            normed.reshape(frames_dev, groups, per_group, width),
            (("frame_0", "frame_1"), "frame_2"),
            (1, 0),
            1,
            0,
        )[:, 0],
        whole_weight,
        preferred_element_type=jnp.float32,
    ).astype(jnp.bfloat16)
    temporal = temporal_mix(local, allowed)[:, None]
    temporal = temporal.reshape(frames_all, per_group, width)
    temporal_out = lax.all_to_all(
        temporal.astype(jnp.bfloat16), FRAME, split_axis=0, concat_axis=1, tiled=True
    ).astype(temporal.dtype)
    return (hidden.reshape(frames_dev, patches_dev, width), temporal_out)


def solution(mesh):
    split = Mesh(
        mesh.devices.reshape(2, 8, 2, mesh.shape["space"]),
        ("frame_0", "frame_1", "frame_2", "space"),
    )
    return jax.shard_map(
        shards,
        mesh=split,
        in_specs=(
            P(FRAME, "space", None),
            P(FRAME, "space", None),
            P(FRAME, "space", None),
            P(FRAME, "space", None),
            P(FRAME, None),
            P(),
            P(),
            P(),
            P(),
            P(FRAME, None),
            P(),
        ),
        out_specs=(P(FRAME, "space", None), P(FRAME, "space", None)),
        check_vma=False,
    )
```

profile of v0, /device:TPU:1, one launch (start us, length us, event | category | flops | bytes accessed | tf_op | source)
XLA Modules:
  0.0 205.7 jit_solution(14141695110795643575)
XLA Ops:
  7.2 0.0 all-gather.5.cloned.1.call-start
  7.2 0.7 all-gather.5.cloned.1.call-update
  7.9 0.0 all-gather.7.cloned.1.call-start
  8.0 0.7 all-gather.7.cloned.1.call-update
  8.7 1.4 reshape.123
  10.0 0.8 copy.88
  10.8 10.2 %all-to-all-start = ((bf16[1,64,16,72]{3,1,0,2:T(8,128)(2,1)}), bf16[1,64,16,72]{3,1,0,2:T(8,128)(2,1)S(1)}, u32[]{:S(2)}, u32[]{:S(2)}) async-start(bf16[1,64,16,72]{3,1,0,2:T(8,128)(2,1)} %copy.88), calls=%async_computation | async-start | bytes 524288 | tf_op jit(solution)/shard_map/all_to_all | solution.py:107
  21.0 1.4 reshape.124
  22.4 0.8 copy.90
  23.2 10.2 %all-to-all-done = bf16[1,64,16,72]{3,1,0,2:T(8,128)(2,1)S(1)} async-done(((bf16[1,64,16,72]{3,1,0,2:T(8,128)(2,1)}), bf16[1,64,16,72]{3,1,0,2:T(8,128)(2,1)S(1)}, u32[]{:S(2)}, u32[]{:S(2)}) %all-to-all-start) | async-done | bytes 147488 | tf_op jit(solution)/shard_map/all_to_all | solution.py:107
  33.4 3.9 %all-to-all-start.1 = ((bf16[1,64,16,72]{3,1,0,2:T(8,128)(2,1)}), bf16[1,64,16,72]{3,1,0,2:T(8,128)(2,1)S(1)}, u32[]{:S(2)}, u32[]{:S(2)}) async-start(bf16[1,64,16,72]{3,1,0,2:T(8,128)(2,1)} %copy.90), calls=%async_computation.1 | async-start | bytes 524288 | tf_op jit(solution)/shard_map/all_to_all | solution.py:108
  37.3 0.5 reshape.125
  37.7 0.8 copy.92
  38.5 13.1 %all-to-all-done.1 = bf16[1,64,16,72]{3,1,0,2:T(8,128)(2,1)S(1)} async-done(((bf16[1,64,16,72]{3,1,0,2:T(8,128)(2,1)}), bf16[1,64,16,72]{3,1,0,2:T(8,128)(2,1)S(1)}, u32[]{:S(2)}, u32[]{:S(2)}) %all-to-all-start.1) | async-done | bytes 147488 | tf_op jit(solution)/shard_map/all_to_all | solution.py:108
  51.6 3.5 %all-to-all-start.2 = ((bf16[1,64,16,72]{3,1,0,2:T(8,128)(2,1)}), bf16[1,64,16,72]{3,1,0,2:T(8,128)(2,1)S(1)}, u32[]{:S(2)}, u32[]{:S(2)}) async-start(bf16[1,64,16,72]{3,1,0,2:T(8,128)(2,1)} %copy.92), calls=%async_computation.2 | async-start | bytes 524288 | tf_op jit(solution)/shard_map/all_to_all | solution.py:111
  55.2 0.1 copy.94
  55.3 0.1 copy.112
  55.4 14.1 %all-to-all-done.2 = bf16[1,64,16,72]{3,1,0,2:T(8,128)(2,1)S(1)} async-done(((bf16[1,64,16,72]{3,1,0,2:T(8,128)(2,1)}), bf16[1,64,16,72]{3,1,0,2:T(8,128)(2,1)S(1)}, u32[]{:S(2)}, u32[]{:S(2)}) %all-to-all-start.2) | async-done | bytes 147488 | tf_op jit(solution)/shard_map/all_to_all | solution.py:111
  69.6 0.1 copy.113
  69.7 3.4 %while.10 = (s32[]{:T(128)}, bf16[2,1,512,1,72]{2,4,3,1,0:T(8,128)(2,1)S(1)}, bf16[2,1,512,1,72]{2,4,3,1,0:T(8,128)(2,1)S(1)}, bf16[1,1024,1,72]{1,3,2,0:T(8,128...) while((s32[]{:T(128)}, bf16[2,1,512,1,72]{2,4,3,1,0:T(8,128)(2,1)S(1)}, ...), condition=%wide.region_3.4_spmd, body=%wide.region_0.3_spmd.sunk | while | flops 155261952 | bytes 6744149 | solution.py:62
  69.7 0.6 multiply_reduce_fusion.3
  70.3 0.5 fusion.39
  70.8 0.6 fusion.40
  71.4 0.5 multiply_reduce_fusion.3
  71.9 0.5 fusion.39
  72.5 0.6 fusion.40
  73.1 0.2 copy.114
  73.3 0.1 reshape.140
  73.4 0.5 broadcast.46
  73.9 2.3 %reduce.5 = bf16[1024,72]{1,0:T(8,128)(2,1)S(1)} reduce(bf16[1024,1,1,72]{3,2,1,0:T(2,128)(2,1)S(1)} %bitcast.98, bf16[]{:T(256)} %broadcast.46), dimensions={1,2}, to_apply=%bitcast.78.reduce_sub_computation | reduce | bytes 294914
  76.2 1.2 reshape.144
  77.4 3.5 %all-to-all-start.3 = ((bf16[16,2,2304]{2,1,0:T(2,128)(2,1)}), bf16[16,2,2304]{2,1,0:T(2,128)(2,1)S(1)}, u32[]{:S(2)}, u32[]{:S(2)}) async-start(bf16[16,2,2304]{2,1,0:T(2,128)(2,1)} %reshape.144), calls=%async_computation.3 | async-start | bytes 294912 | tf_op jit(solution)/shard_map/all_to_all | solution.py:116
  80.9 0.1 copy.102
  81.0 0.1 reduce.4
  81.2 9.5 %all-to-all-done.3 = bf16[16,2,2304]{2,1,0:T(2,128)(2,1)S(1)} async-done(((bf16[16,2,2304]{2,1,0:T(2,128)(2,1)}), bf16[16,2,2304]{2,1,0:T(2,128)(2,1)S(1)}, u32[]{:S(2)}, u32[]{:S(2)}) %all-to-all-start.3) | async-done | bytes 147488 | tf_op jit(solution)/shard_map/all_to_all | solution.py:116
  90.7 0.9 reshape.145
  91.6 0.3 copy.97
  92.0 0.2 all_to_all.73
  92.2 0.4 copy.98
  92.6 0.3 reshape.126
  92.9 3.6 %reshape.136 = bf16[1152,1152]{1,0:T(8,128)(2,1)S(1)} reshape(bf16[32,36,1152]{2,1,0:T(8,128)(2,1)} %all-gather.5.cloned.1.call-done) | data formatting | bytes 5308416
  96.6 0.7 fusion.28
  97.3 0.2 multiply_reduce_fusion.1
  97.5 0.1 add_convert_fusion
  97.6 0.1 reshape_transpose_reshape_reshape.3
  97.7 0.1 copy.99
  97.8 6.7 %all_to_all.85 = bf16[16,2,1,1,2,1152]{5,4,0,3,2,1:T(2,128)(2,1)S(1)} all-to-all(bf16[16,2,1,1,2,1152]{5,4,0,3,2,1:T(2,128)(2,1)S(1)} %copy.99), channel_id=1, replica_groups=mesh['frame_0'=2,'frame_1'=8,'frame_2'=2,'space'=16] {'frame_2'}, dimensions={1} | all-to-all | bytes 294912 | tf_op jit(solution)/shard_map/all_to_all | solution.py:28
  104.5 0.8 copy.100
  105.3 9.1 %all-to-all-start.5 = ((bf16[16,2,1,1,2,1152]{5,4,1,3,2,0:T(2,128)(2,1)}), bf16[16,2,1,1,2,1152]{5,4,1,3,2,0:T(2,128)(2,1)S(1)}, u32[]{:S(2)}, u32[]{:S(2)}) async-start(bf16[16,2,1,1,2,1152]{5,4,1,3,2,0:T(2,128)(2,1)} %copy.100), calls=%async_computation.5 | async-start | bytes 294912 | tf_op jit(solution)/shard_map/all_to_all | solution.py:28
  114.4 0.1 convert_reduce_fusion
  114.5 0.1 broadcast_compare_fusion
  114.6 49.2 %all-gather.7.cloned.1.call-done = bf16[32,36,3456]{2,1,0:T(8,128)(2,1)} async-done(((bf16[1,36,3456]{2,1,0:T(8,128)(2,1)}), bf16[32,36,3456]{2,1,0:T(8,128)(2,1)}) %all-gather.7.cloned.1.call-update) | async-done | bytes 7962640 | tf_op jit(solution)/shard_map/all_gather | solution.py:142
  163.8 12.4 %reshape.139 = bf16[1152,3456,1]{1,0,2:T(8,128)(2,1)} reshape(bf16[32,36,3456]{2,1,0:T(8,128)(2,1)} %all-gather.7.cloned.1.call-done) | data formatting | bytes 15925248
  176.2 4.6 %convolution_convert_fusion = bf16[32,2,3456]{2,0,1:T(8,128)(2,1)S(1)} fusion(bf16[1152,3456,1]{1,0,2:T(8,128)(2,1)} %reshape.139, bf16[32,2,1152]{2,1,0:T(2,128)(2,1)S(1)} %bitcast.104), kind=kOutput, calls=%fused_computation.16 | convolution fusion | flops 509829120 | bytes 8552448 | tf_op jit(solution)/shard_map/fnc,ce->fne/dot_general | solution.py:143
  180.8 0.5 reshape.132
  181.3 0.5 reshape.131
  181.7 0.5 reshape.128
  182.2 0.3 fusion.29
  182.5 0.1 fusion.19
  182.6 0.3 fusion.18
  183.0 0.1 copy.116
  183.1 0.4 reshape.142
  183.5 14.6 %all_to_all.86 = bf16[32,2,1152]{2,1,0:T(2,128)(2,1)S(1)} all-to-all(bf16[32,2,1152]{2,1,0:T(2,128)(2,1)S(1)} %reshape.142), channel_id=1, replica_groups=mesh['frame_0'=2,'frame_1'=8,'frame_2'=2,'space'=16] {'frame_0','frame_1..., dimensions={0} | all-to-all | bytes 294912 | tf_op jit(solution)/shard_map/all_to_all | solution.py:157
  198.1 0.8 reshape.134
  (24 shorter events, 0.2 us)
Async XLA Ops:
  7.2 30.1 %copy-start.1 = (bf16[1,64,1152]{2,1,0:T(8,128)(2,1)S(1)}, bf16[1,64,1152]{2,1,0:T(8,128)(2,1)}, u32[]{:S(2)}) copy-start(bf16[1,64,1152]{2,1,0:T(8,128)(2,1)} %param.15) | copy-start | bytes 442372
  7.2 85.7 %all-gather.5.cloned.1.call-start = ((), (), s32[]{:S(2)}) async-start(), calls=%async_computation.7 | async-start | bytes 3041280 | tf_op jit(solution)/shard_map/all_gather | solution.py:121
  7.9 155.8 %all-gather.7.cloned.1.call-start = ((), (), s32[]{:S(2)}) async-start(), calls=%async_computation.8 | async-start | bytes 9123840 | tf_op jit(solution)/shard_map/all_gather | solution.py:142
  10.8 22.6 %all-to-all-start = ((bf16[1,64,16,72]{3,1,0,2:T(8,128)(2,1)}), bf16[1,64,16,72]{3,1,0,2:T(8,128)(2,1)S(1)}, u32[]{:S(2)}, u32[]{:S(2)}) async-start(bf16[1,64,16,72]{3,1,0,2:T(8,128)(2,1)} %copy.88), calls=%async_computation | async-start | bytes 524288 | tf_op jit(solution)/shard_map/all_to_all | solution.py:107
  33.4 18.2 %all-to-all-start.1 = ((bf16[1,64,16,72]{3,1,0,2:T(8,128)(2,1)}), bf16[1,64,16,72]{3,1,0,2:T(8,128)(2,1)S(1)}, u32[]{:S(2)}, u32[]{:S(2)}) async-start(bf16[1,64,16,72]{3,1,0,2:T(8,128)(2,1)} %copy.90), calls=%async_computation.1 | async-start | bytes 524288 | tf_op jit(solution)/shard_map/all_to_all | solution.py:108
  51.6 18.0 %all-to-all-start.2 = ((bf16[1,64,16,72]{3,1,0,2:T(8,128)(2,1)}), bf16[1,64,16,72]{3,1,0,2:T(8,128)(2,1)S(1)}, u32[]{:S(2)}, u32[]{:S(2)}) async-start(bf16[1,64,16,72]{3,1,0,2:T(8,128)(2,1)} %copy.92), calls=%async_computation.2 | async-start | bytes 524288 | tf_op jit(solution)/shard_map/all_to_all | solution.py:111
  73.1 7.8 %copy-start.7 = (s32[16]{0:T(128)S(1)}, s32[16]{0:T(128)}, u32[]{:S(2)}) copy-start(s32[16]{0:T(128)} %param.23) | copy-start | bytes 196
  73.1 8.1 %copy-start.6 = (f32[1152]{0:T(1024)S(1)}, f32[1152]{0:T(1024)}, u32[]{:S(2)}) copy-start(f32[1152]{0:T(1024)} %param.21) | copy-start | bytes 13828
  77.4 13.3 %all-to-all-start.3 = ((bf16[16,2,2304]{2,1,0:T(2,128)(2,1)}), bf16[16,2,2304]{2,1,0:T(2,128)(2,1)S(1)}, u32[]{:S(2)}, u32[]{:S(2)}) async-start(bf16[16,2,2304]{2,1,0:T(2,128)(2,1)} %reshape.144), calls=%async_computation.3 | async-start | bytes 294912 | tf_op jit(solution)/shard_map/all_to_all | solution.py:116
  92.8 3.7 %copy-start.2 = (bf16[1,64,1152]{2,1,0:T(8,128)(2,1)S(1)}, bf16[1,64,1152]{2,1,0:T(8,128)(2,1)}, u32[]{:S(2)}) copy-start(bf16[1,64,1152]{2,1,0:T(8,128)(2,1)} %param.16) | copy-start | bytes 442372
  92.9 3.7 %copy-start.3 = (f32[1152]{0:T(1024)S(1)}, f32[1152]{0:T(1024)}, u32[]{:S(2)}) copy-start(f32[1152]{0:T(1024)} %param.18) | copy-start | bytes 13828
  92.9 3.7 %copy-start.4 = (f32[1152]{0:T(1024)S(1)}, f32[1152]{0:T(1024)}, u32[]{:S(2)}) copy-start(f32[1152]{0:T(1024)} %param.19) | copy-start | bytes 13828
  96.6 0.9 copy-start.5
  97.3 78.9 %copy-start = (f32[64,1152]{1,0:T(8,128)}, f32[64,1152]{1,0:T(8,128)S(1)}, u32[]{:S(2)}) copy-start(f32[64,1152]{1,0:T(8,128)S(1)} %get-tuple-element.71) | copy-start | bytes 884740
  105.3 70.9 %all-to-all-start.5 = ((bf16[16,2,1,1,2,1152]{5,4,1,3,2,0:T(2,128)(2,1)}), bf16[16,2,1,1,2,1152]{5,4,1,3,2,0:T(2,128)(2,1)S(1)}, u32[]{:S(2)}, u32[]{:S(2)}) async-start(bf16[16,2,1,1,2,1152]{5,4,1,3,2,0:T(2,128)(2,1)} %copy.100), calls=%async_computation.5 | async-start | bytes 294912 | tf_op jit(solution)/shard_map/all_to_all | solution.py:28
Sparse Core Ops, SparseCore 0:
  10.1 74.3 all-gather.4
  86.6 77.0 all-gather.6
where the time goes:
time: 207 us; the launch traced here: 206 us
  waiting for transfers between devices  97.6 us (47%)
  starting transfers between devices  30.3 us (15%)
  local copies, waits for them, and re-layouts  29.8 us (14%)
  blocking collectives  21.3 us (10%)
  between operations  14.4 us (7%)
  matrix products  8.13 us (4%)
  other arithmetic  4.11 us (2%)
    all_gather x1, waiting for transfers between devices, shards(): whole_weight = lax.all_gather(temporal_weight, FRAME, axis=0, tiled=True)  49.2 us
    unnamed x21, local copies, waits for them, and re-layouts  18.7 us
    all_to_all x1, blocking collectives, shards(): lax.all_to_all(temporal.astype(jnp.bfloat16), FRAME, split_axis=0, concat...  14.6 us
    all_to_all x1, waiting for transfers between devices, shards(): lax.all_to_all(spatial_value.reshape(split), 'space', split_axis=2, conca...  14.1 us
    all_to_all x1, waiting for transfers between devices, shards(): lax.all_to_all(spatial_key.reshape(split), 'space', split_axis=2, concat_...  13.1 us
    all_to_all x1, starting transfers between devices, shards(): lax.all_to_all(query, 'space', split_axis=2, concat_axis=1, tiled=True)  10.2 us
    all_to_all x1, waiting for transfers between devices, shards(): lax.all_to_all(query, 'space', split_axis=2, concat_axis=1, tiled=True)  10.2 us
    all_to_all x1, waiting for transfers between devices, shards(): lax.all_to_all(mixed_heads, 'space', split_axis=1, concat_axis=2, tiled=T...  9.53 us
  transfers between devices with their start and end apart: 7, of which 5 were waited for; matrix products, arithmetic and copies ran while one was open for 16% of the time, Pallas kernels for 0%

commit v1 on v0

--- a/solution.py
+++ b/solution.py
@@ -139,7 +139,9 @@
         axis=1,
     )
     allowed = clip_of[:, None] == clip_of[None, :]
-    whole_weight = lax.all_gather(temporal_weight, FRAME, axis=0, tiled=True)
+    whole_weight = jnp.concatenate(
+        lax.all_to_all(jnp.stack([temporal_weight] * lax.axis_size(FRAME)), FRAME, 0, 0), axis=0
+    )
     local = jnp.einsum(
         "fnc,ce->fne",
         exchange_by_chip(

time: 207 us -> 382 us (1.85)
  waiting for transfers between devices: 97.6 us -> 253 us
  starting transfers between devices: 30.3 us -> 43.7 us
  local copies, waits for them, and re-layouts: 29.8 us -> 33.8 us
    all_to_all x0 -> x1, waiting for transfers between devices: none -> 205 us  [shards(): lax.all_to_all(jnp.stack([temporal_weight] * lax.axis_size(FRAME)), FRAME...]
    all_gather x1 -> x0, waiting for transfers between devices: 49.2 us -> none  [shards(): whole_weight = lax.all_gather(temporal_weight, FRAME, axis=0, tiled=True)]
    reshape x0 -> x1, local copies, waits for them, and re-layouts: none -> 12.4 us  [shards(): jnp.concatenate(lax.all_to_all(jnp.stack([temporal_weight] * lax.axis_siz...]
    unnamed x21 -> x22, local copies, waits for them, and re-layouts: 18.7 us -> 6.26 us
    all_to_all x0 -> x1, starting transfers between devices: none -> 11.2 us  [shards(): lax.all_to_all(jnp.stack([temporal_weight] * lax.axis_size(FRAME)), FRAME...]
    another operation x1 -> x2, local copies, waits for them, and re-layouts: 0.08 us -> 4.09 us  [the longest x1 4 us: shards(): jnp.stack([temporal_weight] * lax.axis_size(FRAME))]
  transfers between devices with their start and end apart: 7 -> 7, of which waited for: 5 -> 5; matrix products, arithmetic and copies ran while one was open for 16% -> 8% of each run, Pallas kernels for 0% -> 0%
where the time goes in v1:
time: 382 us; the launch traced here: 381 us
  waiting for transfers between devices  253 us (66%)
  starting transfers between devices  43.7 us (11%)
  local copies, waits for them, and re-layouts  33.8 us (9%)
  blocking collectives  23.8 us (6%)
  between operations  14.4 us (4%)
  matrix products  8.13 us (2%)
  other arithmetic  4.11 us (1%)
    all_to_all x1, waiting for transfers between devices, shards(): lax.all_to_all(jnp.stack([temporal_weight] * lax.axis_size(FRAME)), FRAME...  205 us
    all_to_all x1, blocking collectives, shards(): lax.all_to_all(temporal.astype(jnp.bfloat16), FRAME, split_axis=0, concat...  17.5 us
    all_to_all x1, waiting for transfers between devices, shards(): lax.all_to_all(spatial_value.reshape(split), 'space', split_axis=2, conca...  14.4 us
    all_to_all x1, waiting for transfers between devices, shards(): lax.all_to_all(spatial_key.reshape(split), 'space', split_axis=2, concat_...  12.5 us
    reshape x1, local copies, waits for them, and re-layouts, shards(): jnp.concatenate(lax.all_to_all(jnp.stack([temporal_weight] * lax.axis_siz...  12.4 us
    all_to_all x1, starting transfers between devices, exchange_in_order(): lax.all_to_all(blocks, axes[k], split_axis=k, concat_axis=k, tiled=True)  11.3 us
    all_to_all x1, starting transfers between devices, shards(): lax.all_to_all(jnp.stack([temporal_weight] * lax.axis_size(FRAME)), FRAME...  11.2 us
    all_to_all x1, starting transfers between devices, shards(): lax.all_to_all(query, 'space', split_axis=2, concat_axis=1, tiled=True)  10.2 us
  transfers between devices with their start and end apart: 7, of which 5 were waited for; matrix products, arithmetic and copies ran while one was open for 8% of the time, Pallas kernels for 0%

profile of v1, /device:TPU:1, one launch (start us, length us, event | category | flops | bytes accessed | tf_op | source)
XLA Modules:
  0.0 380.6 jit_solution(4945488893608150947)
XLA Ops:
  7.2 0.0 all-gather.3.cloned.1.call-start
  7.2 0.7 all-gather.3.cloned.1.call-update
  7.9 1.4 reshape.128
  9.3 0.8 copy.88
  10.1 10.2 %all-to-all-start = ((bf16[1,64,16,72]{3,1,0,2:T(8,128)(2,1)}), bf16[1,64,16,72]{3,1,0,2:T(8,128)(2,1)S(1)}, u32[]{:S(2)}, u32[]{:S(2)}) async-start(bf16[1,64,16,72]{3,1,0,2:T(8,128)(2,1)} %copy.88), calls=%async_computation | async-start | bytes 524288 | tf_op jit(solution)/shard_map/all_to_all | solution.py:107
  20.3 1.4 reshape.129
  21.7 0.8 copy.90
  22.4 10.2 %all-to-all-done = bf16[1,64,16,72]{3,1,0,2:T(8,128)(2,1)S(1)} async-done(((bf16[1,64,16,72]{3,1,0,2:T(8,128)(2,1)}), bf16[1,64,16,72]{3,1,0,2:T(8,128)(2,1)S(1)}, u32[]{:S(2)}, u32[]{:S(2)}) %all-to-all-start) | async-done | bytes 147488 | tf_op jit(solution)/shard_map/all_to_all | solution.py:107
  32.6 3.9 %all-to-all-start.1 = ((bf16[1,64,16,72]{3,1,0,2:T(8,128)(2,1)}), bf16[1,64,16,72]{3,1,0,2:T(8,128)(2,1)S(1)}, u32[]{:S(2)}, u32[]{:S(2)}) async-start(bf16[1,64,16,72]{3,1,0,2:T(8,128)(2,1)} %copy.90), calls=%async_computation.1 | async-start | bytes 524288 | tf_op jit(solution)/shard_map/all_to_all | solution.py:108
  36.5 0.5 reshape.130
  37.0 0.8 copy.92
  37.8 12.5 %all-to-all-done.1 = bf16[1,64,16,72]{3,1,0,2:T(8,128)(2,1)S(1)} async-done(((bf16[1,64,16,72]{3,1,0,2:T(8,128)(2,1)}), bf16[1,64,16,72]{3,1,0,2:T(8,128)(2,1)S(1)}, u32[]{:S(2)}, u32[]{:S(2)}) %all-to-all-start.1) | async-done | bytes 147488 | tf_op jit(solution)/shard_map/all_to_all | solution.py:108
  50.3 3.5 all-to-all-start.2
  53.8 0.1 copy.94
  53.9 0.1 copy.112
  54.1 14.4 %all-to-all-done.2 = bf16[1,64,16,72]{3,1,0,2:T(8,128)(2,1)S(1)} async-done(((bf16[1,64,16,72]{3,1,0,2:T(8,128)(2,1)}), bf16[1,64,16,72]{3,1,0,2:T(8,128)(2,1)S(1)}, u32[]{:S(2)}, u32[]{:S(2)}) %all-to-all-start.2) | async-done | bytes 147488 | tf_op jit(solution)/shard_map/all_to_all | solution.py:111
  68.5 0.1 copy.113
  68.6 3.4 while.10
  68.6 0.6 multiply_reduce_fusion.3
  69.2 0.5 fusion.39
  69.7 0.6 fusion.40
  70.3 0.5 multiply_reduce_fusion.3
  70.8 0.5 fusion.39
  71.4 0.6 fusion.40
  72.0 0.2 copy.114
  72.1 0.1 reshape.144
  72.3 0.5 broadcast.48
  72.8 2.3 reduce.5
  75.1 1.2 reshape.148
  76.3 3.5 all-to-all-start.3
  79.8 9.8 %all-to-all-done.3 = bf16[16,2,2304]{2,1,0:T(2,128)(2,1)S(1)} async-done(((bf16[16,2,2304]{2,1,0:T(2,128)(2,1)}), bf16[16,2,2304]{2,1,0:T(2,128)(2,1)S(1)}, u32[]{:S(2)}, u32[]{:S(2)}) %all-to-all-start.3) | async-done | bytes 147488 | tf_op jit(solution)/shard_map/all_to_all | solution.py:116
  89.6 0.9 reshape.149
  90.6 0.3 copy.97
  90.9 0.2 all_to_all.76
  91.1 0.4 copy.98
  91.5 0.3 reshape.131
  91.8 3.6 reshape.142
  95.5 0.7 fusion.28
  96.2 0.2 multiply_reduce_fusion.1
  96.5 0.1 add_convert_fusion
  96.6 0.1 reshape_transpose_reshape_reshape.3
  96.6 0.1 copy.99
  96.8 6.3 %all_to_all.90 = bf16[16,2,1,1,2,1152]{5,4,0,3,2,1:T(2,128)(2,1)S(1)} all-to-all(bf16[16,2,1,1,2,1152]{5,4,0,3,2,1:T(2,128)(2,1)S(1)} %copy.99), channel_id=1, replica_groups=mesh['frame_0'=2,'frame_1'=8,'frame_2'=2,'space'=16] {'frame_2'}, dimensions={1} | all-to-all | bytes 294912 | tf_op jit(solution)/shard_map/all_to_all | solution.py:28
  103.0 4.0 %stack.2 = bf16[32,36,3456]{2,1,0:T(8,128)(2,1)} broadcast(bf16[36,3456]{1,0:T(8,128)(2,1)S(1)} %copy-done.1), dimensions={1,2} | broadcast | bytes 8211456 | tf_op jit(solution)/shard_map/stack | solution.py:143
  107.1 11.2 %all-to-all-start.6 = ((bf16[32,36,3456]{2,1,0:T(8,128)(2,1)}), bf16[32,36,3456]{2,1,0:T(8,128)(2,1)}, u32[]{:S(2)}, u32[]{:S(2)}) async-start(bf16[32,36,3456]{2,1,0:T(8,128)(2,1)} %stack.2), calls=%async_computation.6 | async-start | bytes 17694720 | tf_op jit(solution)/shard_map/all_to_all | solution.py:143
  118.3 0.1 copy.102
  118.4 0.1 reduce.4
  118.6 0.8 copy.100
  119.3 204.9 %all-to-all-done.6 = bf16[32,36,3456]{2,1,0:T(8,128)(2,1)} async-done(((bf16[32,36,3456]{2,1,0:T(8,128)(2,1)}), bf16[32,36,3456]{2,1,0:T(8,128)(2,1)}, u32[]{:S(2)}, u32[]{:S(2)}) %all-to-all-start.6) | async-done | bytes 7962656 | tf_op jit(solution)/shard_map/all_to_all | solution.py:143
  324.2 11.3 %all-to-all-start.5 = ((bf16[16,2,1,1,2,1152]{5,4,1,3,2,0:T(2,128)(2,1)}), bf16[16,2,1,1,2,1152]{5,4,1,3,2,0:T(2,128)(2,1)S(1)}, u32[]{:S(2)}, u32[]{:S(2)}) async-start(bf16[16,2,1,1,2,1152]{5,4,1,3,2,0:T(2,128)(2,1)} %copy.100), calls=%async_computation.5 | async-start | bytes 294912 | tf_op jit(solution)/shard_map/all_to_all | solution.py:28
  335.5 0.1 convert_reduce_fusion
  335.6 0.1 broadcast_compare_fusion
  335.7 12.4 %reshape.143 = bf16[1152,3456,1]{1,0,2:T(8,128)(2,1)} reshape(bf16[32,36,3456]{2,1,0:T(8,128)(2,1)} %all-to-all-done.6) | data formatting | bytes 15925248 | tf_op jit(solution)/shard_map/reshape | solution.py:142
  348.1 4.6 %convolution_convert_fusion = bf16[32,2,3456]{2,0,1:T(8,128)(2,1)S(1)} fusion(bf16[1152,3456,1]{1,0,2:T(8,128)(2,1)} %reshape.143, bf16[32,2,1152]{2,1,0:T(2,128)(2,1)S(1)} %bitcast.103), kind=kOutput, calls=%fused_computation.16 | convolution fusion | flops 509829120 | bytes 8552448 | tf_op jit(solution)/shard_map/fnc,ce->fne/dot_general | solution.py:145
  352.8 0.5 reshape.138
  353.2 0.5 reshape.137
  353.7 0.5 reshape.134
  354.2 0.3 fusion.29
  354.5 0.1 fusion.19
  354.6 0.3 fusion.18
  354.9 0.1 copy.116
  355.0 0.4 reshape.146
  355.5 17.5 %all_to_all.91 = bf16[32,2,1152]{2,1,0:T(2,128)(2,1)S(1)} all-to-all(bf16[32,2,1152]{2,1,0:T(2,128)(2,1)S(1)} %reshape.146), channel_id=1, replica_groups=mesh['frame_0'=2,'frame_1'=8,'frame_2'=2,'space'=16] {'frame_0','frame_1..., dimensions={0} | all-to-all | bytes 294912 | tf_op jit(solution)/shard_map/all_to_all | solution.py:159
  373.0 0.8 reshape.140
  (26 shorter events, 0.2 us)
Async XLA Ops:
  7.2 29.3 %copy-start.2 = (bf16[1,64,1152]{2,1,0:T(8,128)(2,1)S(1)}, bf16[1,64,1152]{2,1,0:T(8,128)(2,1)}, u32[]{:S(2)}) copy-start(bf16[1,64,1152]{2,1,0:T(8,128)(2,1)} %param.15) | copy-start | bytes 442372
  7.2 84.7 %all-gather.3.cloned.1.call-start = ((), (), s32[]{:S(2)}) async-start(), calls=%async_computation.8 | async-start | bytes 3041280 | tf_op jit(solution)/shard_map/all_gather | solution.py:121
  10.1 22.6 %all-to-all-start = ((bf16[1,64,16,72]{3,1,0,2:T(8,128)(2,1)}), bf16[1,64,16,72]{3,1,0,2:T(8,128)(2,1)S(1)}, u32[]{:S(2)}, u32[]{:S(2)}) async-start(bf16[1,64,16,72]{3,1,0,2:T(8,128)(2,1)} %copy.88), calls=%async_computation | async-start | bytes 524288 | tf_op jit(solution)/shard_map/all_to_all | solution.py:107
  32.6 17.6 %all-to-all-start.1 = ((bf16[1,64,16,72]{3,1,0,2:T(8,128)(2,1)}), bf16[1,64,16,72]{3,1,0,2:T(8,128)(2,1)S(1)}, u32[]{:S(2)}, u32[]{:S(2)}) async-start(bf16[1,64,16,72]{3,1,0,2:T(8,128)(2,1)} %copy.90), calls=%async_computation.1 | async-start | bytes 524288 | tf_op jit(solution)/shard_map/all_to_all | solution.py:108
  50.3 18.2 %all-to-all-start.2 = ((bf16[1,64,16,72]{3,1,0,2:T(8,128)(2,1)}), bf16[1,64,16,72]{3,1,0,2:T(8,128)(2,1)S(1)}, u32[]{:S(2)}, u32[]{:S(2)}) async-start(bf16[1,64,16,72]{3,1,0,2:T(8,128)(2,1)} %copy.92), calls=%async_computation.2 | async-start | bytes 524288 | tf_op jit(solution)/shard_map/all_to_all | solution.py:111
  71.9 7.8 %copy-start.7 = (f32[1152]{0:T(1024)S(1)}, f32[1152]{0:T(1024)}, u32[]{:S(2)}) copy-start(f32[1152]{0:T(1024)} %param.21) | copy-start | bytes 13828
  76.3 13.4 %all-to-all-start.3 = ((bf16[16,2,2304]{2,1,0:T(2,128)(2,1)}), bf16[16,2,2304]{2,1,0:T(2,128)(2,1)S(1)}, u32[]{:S(2)}, u32[]{:S(2)}) async-start(bf16[16,2,2304]{2,1,0:T(2,128)(2,1)} %reshape.148), calls=%async_computation.3 | async-start | bytes 294912 | tf_op jit(solution)/shard_map/all_to_all | solution.py:116
  91.8 3.7 copy-start.3
  91.8 3.7 copy-start.4
  91.8 3.7 copy-start.5
  95.5 0.9 copy-start.6
  95.5 7.5 %copy-start.1 = (bf16[36,3456]{1,0:T(8,128)(2,1)S(1)}, bf16[36,3456]{1,0:T(8,128)(2,1)}, u32[]{:S(2)}) copy-start(bf16[36,3456]{1,0:T(8,128)(2,1)} %param.22) | copy-start | bytes 746500
  96.2 10.8 %copy-start = (f32[64,1152]{1,0:T(8,128)}, f32[64,1152]{1,0:T(8,128)S(1)}, u32[]{:S(2)}) copy-start(f32[64,1152]{1,0:T(8,128)S(1)} %get-tuple-element.71) | copy-start | bytes 884740
  107.1 11.3 %copy-start.8 = (s32[16]{0:T(128)S(1)}, s32[16]{0:T(128)}, u32[]{:S(2)}) copy-start(s32[16]{0:T(128)} %param.23) | copy-start | bytes 196
  107.1 217.2 %all-to-all-start.6 = ((bf16[32,36,3456]{2,1,0:T(8,128)(2,1)}), bf16[32,36,3456]{2,1,0:T(8,128)(2,1)}, u32[]{:S(2)}, u32[]{:S(2)}) async-start(bf16[32,36,3456]{2,1,0:T(8,128)(2,1)} %stack.2), calls=%async_computation.6 | async-start | bytes 17694720 | tf_op jit(solution)/shard_map/all_to_all | solution.py:143
  324.2 23.9 %all-to-all-start.5 = ((bf16[16,2,1,1,2,1152]{5,4,1,3,2,0:T(2,128)(2,1)}), bf16[16,2,1,1,2,1152]{5,4,1,3,2,0:T(2,128)(2,1)S(1)}, u32[]{:S(2)}, u32[]{:S(2)}) async-start(bf16[16,2,1,1,2,1152]{5,4,1,3,2,0:T(2,128)(2,1)} %copy.100), calls=%async_computation.5 | async-start | bytes 294912 | tf_op jit(solution)/shard_map/all_to_all | solution.py:28
Sparse Core Ops, SparseCore 0:
  10.1 74.1 all-gather.2
